TPU v7x, 32 devices: a whole 2x2x4 slice. The times are simulated.
32 devices in a mesh: ep: 8 (over y, x, core), tp: 4 (over z).
Axes of the slice: x: 2, y: 2, z: 4, core: 2. Of those that a mesh axis runs over, the one named last changes fastest.
Arguments:
- tokens: bfloat16 [512, 7168], P('ep'), may hold values from -6 to 6
- gate_scores: float32 [512, 8], P('ep'), may hold values from 0.1 to 1
- expert_ids: int32 [512, 8], P('ep'), may hold values from 0 to 15, all different within a row; in each aligned block of 64 rows (0 to 63, 64 to 127, ...) at most 48 rows name the same one
- gate_weight: bfloat16 [16, 7168, 2048], P('ep', None, 'tp'), may hold values from -0.0625 to 0.0625
- up_weight: bfloat16 [16, 7168, 2048], P('ep', None, 'tp'), may hold values from -0.0625 to 0.0625
- down_weight: bfloat16 [16, 2048, 7168], P('ep', 'tp'), may hold values from -0.125 to 0.125
Outputs:
- mixed: bfloat16 [512, 7168], P('ep', 'tp')
Inputs may be any that keep to these rules, and one draw needn't show every extreme that they name: `expert_ids`: each row names 8 different experts. Among the tokens of one group, no expert is named by more than 48 tokens, and in every draw some expert is named by exactly 48 of them.
All inputs are finite; a program needn't handle non-finite values.
Results may differ from a plain program's by a relative error of at most 0.02.
Values may be sent and summed in bfloat16 or wider, within the bound.
No kernel may reach another device: no remote copies, remote signals or barrier semaphores. Data moves between devices by JAX's collectives and lax.ppermute only.
A program may use at most 192 MiB of HBM per device.

v0:
```python
import jax
import jax.numpy as jnp
from jax import lax
from jax.sharding import PartitionSpec as P


def local(tokens, gate_scores, expert_ids, gate_weight, up_weight, down_weight):
    n_ep = lax.axis_size("ep")
    n_tp = lax.axis_size("tp")
    tok_count, width = tokens.shape
    choose = expert_ids.shape[1]
    exp_local = gate_weight.shape[0]
    experts = exp_local * n_ep
    capacity = min(tok_count, 3 * tok_count * choose // (2 * experts))
    share = width // n_tp
    expert_range = jnp.arange(experts)
    picked = jnp.sum(
        (expert_ids[:, :, None] == expert_range[None, None, :]).astype(jnp.int32), axis=1
    )
    rank = jnp.cumsum(picked, axis=0) - picked
    slot = jnp.take_along_axis(rank, expert_ids, axis=1)
    token_range = jnp.arange(tok_count)
    slot_range = jnp.arange(capacity)
    hits = (rank.T[:, None, :] == slot_range[None, :, None]) & (picked.T[:, None, :] > 0)
    found = jnp.any(hits, axis=2)
    index = jnp.where(
        found, jnp.sum(hits.astype(jnp.int32) * token_range[None, None, :], axis=2), tok_count
    )
    padded = jnp.concatenate([tokens, jnp.zeros((1, width), jnp.bfloat16)], axis=0)
    outgoing = padded[index].reshape(n_ep, exp_local, capacity, width)
    received = lax.all_to_all(outgoing, "ep", split_axis=0, concat_axis=0, tiled=True)
    gate = jnp.einsum("sjcd,jdf->sjcf", received, gate_weight, preferred_element_type=jnp.float32)
    upper = jnp.einsum("sjcd,jdf->sjcf", received, up_weight, preferred_element_type=jnp.float32)
    hidden = (jax.nn.silu(gate) * upper).astype(jnp.bfloat16)
    partial_value = jnp.einsum(
        "sjcf,jfd->sjcd", hidden, down_weight, preferred_element_type=jnp.float32
    )
    rounded = partial_value.astype(jnp.bfloat16)
    summed = (
        lax.psum_scatter(rounded, "tp", scatter_dimension=3, tiled=True)
        .astype(jnp.float32)
        .astype(jnp.bfloat16)
    )
    returned = lax.all_to_all(summed, "ep", split_axis=0, concat_axis=0, tiled=True)
    results = returned.reshape(experts * capacity, share)
    flat_index = expert_ids * capacity + slot
    chosen_rows = results[flat_index]
    weights = 2.5 * gate_scores / jnp.sum(gate_scores, axis=1, keepdims=True)
    mixed = jnp.einsum("tk,tkd->td", weights, chosen_rows.astype(jnp.float32))
    return mixed.astype(jnp.bfloat16)


def solution(mesh):
    placed = (
        P("ep", None),
        P("ep", None),
        P("ep", None),
        P("ep", None, "tp"),
        P("ep", None, "tp"),
        P("ep", "tp", None),
    )
    return jax.shard_map(
        local, mesh=mesh, in_specs=placed, out_specs=P("ep", "tp"), check_vma=False
    )
```

profile of v0, /device:TPU:0, one launch (start us, length us, event | category | flops | bytes accessed | tf_op | source)
XLA Modules:
  0.0 418.8 jit_solution(12055357871420945862)
XLA Ops:
  6.5 0.0 reduce-scatter.2.cloned.1.call-start
  6.5 0.7 convert_reduce_fusion
  7.2 0.1 copy.48
  7.3 0.1 reduce_window_sum.11
  7.4 0.1 copy.50
  7.5 0.4 select_reduce_fusion
  7.9 0.4 fusion.25
  8.2 0.1 reshape.47
  8.3 1.2 concatenate.3
  9.6 9.5 %gather_fusion = bf16[768,7168]{1,0:T(8,128)(2,1)} fusion(bf16[65,7168]{1,0:T(8,128)(2,1)S(1)} %concatenate.3, s32[1024]{0:T(1024)S(1)} %pad_clamp_fusion.1), kind=kCustom, calls=%fused_computation | custom fusion | bytes 22023168 | tf_op jit(solution)/shard_map/gather | solution.py:30
  19.0 127.3 %all_to_all.10 = bf16[8,2,48,7168]{3,2,1,0:T(8,128)(2,1)S(1)} all-to-all(bf16[8,2,48,7168]{3,2,1,0:T(8,128)(2,1)} %bitcast.65), channel_id=1, replica_groups=mesh['ep'=8,'tp'=4] {'ep'}, dimensions={0} | all-to-all | bytes 22020096 | tf_op jit(solution)/shard_map/all_to_all | solution.py:31
  146.3 9.1 %fusion.2 = f32[2,8,48,512]{3,2,1,0:T(8,128)S(1)} fusion(bf16[2,7168,512]{2,1,0:T(8,128)(2,1)} %param.10, bf16[8,2,48,7168]{3,2,1,0:T(8,128)(2,1)S(1)} %all_to_all.10), kind=kOutput, calls=%fused_computation.5 | convolution fusion | flops 5637144576 | bytes 27262976 | tf_op jit(solution)/shard_map/sjcd,jdf->sjcf/dot_general | solution.py:33
  155.4 9.5 %fusion.16 = bf16[8,2,48,512]{3,2,0,1:T(8,128)(2,1)S(1)} fusion(f32[2,8,48,512]{3,2,1,0:T(8,128)S(1)} %fusion.2, bf16[2,7168,512]{2,1,0:T(8,128)(2,1)} %param.9, bf16[8,2,48,7168]{3,2,1,0:T(8,128)(2,1)S(1)} %all_to_all.10), kind=kOutput, calls=%fused_computation.16 | convolution fusion | flops 5639503872 | bytes 28049408 | tf_op jit(solution)/shard_map/sjcd,jdf->sjcf/dot_general | solution.py:32
  165.0 13.9 %fusion.9 = bf16[8,2,48,7168]{3,2,0,1:T(8,128)(2,1)} fusion(bf16[8,2,48,512]{3,2,0,1:T(8,128)(2,1)S(1)} %fusion.16, bf16[2,512,7168]{2,1,0:T(8,128)(2,1)} %param.11), kind=kOutput, calls=%fused_computation.10 | convolution fusion | flops 5642649600 | bytes 26476544 | tf_op jit(solution)/shard_map/sjcf,jfd->sjcd/dot_general | solution.py:35
  178.9 0.0 copy-start
  178.9 0.0 reduce-scatter.2.cloned.1.call-update
  178.9 186.2 %reduce-scatter.2.cloned.1.call-done = bf16[8,2,48,1792]{3,2,0,1:T(8,128)(2,1)} async-done(((bf16[8,2,48,7168]{3,2,0,1:T(8,128)(2,1)}), bf16[8,2,48,1792]{3,2,0,1:T(8,128)(2,1)}) %reduce-scatter.2.cloned.1.call-update) | async-done | bytes 2752528 | tf_op jit(solution)/shard_map/reduce_scatter | solution.py:40
  365.1 3.5 copy.53
  368.6 3.7 all-to-all-start.1
  372.3 0.0 copy-done
  372.3 0.1 copy.54
  372.4 0.1 reshape.61
  372.5 0.0 copy-start.1
  372.5 3.8 gather_fusion.2
  376.2 0.1 reshape.64
  376.3 0.1 copy.55
  376.4 0.1 copy.56
  376.5 0.1 reshape.55
  376.6 0.0 copy-done.1
  376.6 0.1 copy.60
  376.8 29.1 %all-to-all-done.1 = bf16[8,2,48,1792]{3,2,1,0:T(8,128)(2,1)S(1)} async-done(((bf16[8,2,48,1792]{3,2,1,0:T(8,128)(2,1)}), bf16[8,2,48,1792]{3,2,1,0:T(8,128)(2,1)S(1)}, u32[]{:S(2)}, u32[]{:S(2)}) %all-to-all-start.1) | async-done | bytes 2752544 | tf_op jit(solution)/shard_map/all_to_all | solution.py:44
  405.9 3.2 gather_fusion.1
  409.1 2.1 fusion.14
  411.2 0.7 copy.69
  (9 shorter events, 0.1 us)
Async XLA Ops:
  6.5 358.5 %reduce-scatter.2.cloned.1.call-start = ((), (), s32[]{:S(2)}) async-start(), calls=%async_computation.3 | async-start | bytes 13762560 | tf_op jit(solution)/shard_map/reduce_scatter | solution.py:40
  178.9 193.4 %copy-start = (s32[64,8]{0,1:T(8,128)S(1)}, s32[64,8]{0,1:T(8,128)}, u32[]{:S(2)}) copy-start(s32[64,8]{0,1:T(8,128)} %param.8) | copy-start | bytes 6148
  368.6 37.3 %all-to-all-start.1 = ((bf16[8,2,48,1792]{3,2,1,0:T(8,128)(2,1)}), bf16[8,2,48,1792]{3,2,1,0:T(8,128)(2,1)S(1)}, u32[]{:S(2)}, u32[]{:S(2)}) async-start(bf16[8,2,48,1792]{3,2,1,0:T(8,128)(2,1)} %copy.53), calls=%async_computation.2 | async-start | bytes 5505024 | tf_op jit(solution)/shard_map/all_to_all | solution.py:44
  372.5 4.1 copy-start.1
Sparse Core Ops, SparseCore 0:
  179.0 186.0 reduce-scatter.1
where the time goes:
time: 419 us
  waiting for transfers between devices  215 us (51%)
  blocking collectives  127 us (30%)
  matrix products  34.7 us (8%)
  local copies, waits for them, and re-layouts  22.7 us (5%)
  between operations  13.5 us (3%)
    reduce_scatter x1, waiting for transfers between devices, local(): lax.psum_scatter(rounded, 'tp', scatter_dimension=3, tiled=True)  186 us
    all_to_all x1, blocking collectives, local(): lax.all_to_all(outgoing, 'ep', split_axis=0, concat_axis=0, tiled=True)  127 us
    all_to_all x1, waiting for transfers between devices, local(): lax.all_to_all(summed, 'ep', split_axis=0, concat_axis=0, tiled=True)  29.1 us
    dot_general x1, matrix products, local(): jnp.einsum('sjcf,jfd->sjcd', hidden, down_weight, preferred_element_type=...  13.9 us
    dot_general x1, matrix products, local(): jnp.einsum('sjcd,jdf->sjcf', received, gate_weight, preferred_element_typ...  9.55 us
    gather x1, local copies, waits for them, and re-layouts, local(): outgoing = padded[index].reshape(n_ep, exp_local, capacity, width)  9.46 us
    dot_general x1, matrix products, local(): jnp.einsum('sjcd,jdf->sjcf', received, up_weight, preferred_element_type=...  9.1 us
  transfers between devices with their start and end apart: 2, of which 2 were waited for; matrix products, arithmetic and copies ran while one was open for 1% of the time, Pallas kernels for 0%

commit v1 on v0

v1 whole, which is shorter than its diff:
```python
import functools
import jax
import jax.numpy as jnp
from jax import lax
from jax.experimental import pallas as pl
from jax.experimental.pallas import tpu as pltpu
from jax.sharding import PartitionSpec as P

CHUNKS = 2


def tile_of(size, want):
    tile = min(size, want)
    while size % tile:
        tile -= 128
    return tile


def expert_kernel(counts, groups, k_steps, d_steps, *refs):
    pieces = refs[: len(counts)]
    scale, gate_w, up_w, down_w = refs[len(counts) : len(counts) + 4]
    outs = refs[len(counts) + 4 : len(counts) + 4 + len(groups)]
    gate_acc, up_acc, hidden = refs[len(counts) + 4 + len(groups) :]
    step = pl.program_id(0)
    exp_local, _, ff = gate_w.shape

    @pl.when(step < k_steps)
    def _():
        rows = jnp.concatenate([p[...] for p in pieces], axis=0)
        for e in range(exp_local):
            for acc, weight in ((gate_acc, gate_w), (up_acc, up_w)):
                product = jnp.dot(rows, weight[e], preferred_element_type=jnp.float32)

                @pl.when(step == 0)
                def _():
                    acc[e] = product

                @pl.when(step > 0)
                def _():
                    acc[e] += product

    @pl.when(step == k_steps - 1)
    def _():
        for e in range(exp_local):
            gate = gate_acc[e]
            value = gate / (1.0 + jnp.exp(-gate)) * up_acc[e] * scale[:, e : e + 1]
            hidden[:, e * ff : (e + 1) * ff] = value.astype(jnp.bfloat16)

    @pl.when(step >= k_steps)
    def _():
        down = down_w[...].reshape(exp_local * ff, down_w.shape[2])
        first = 0
        for out, rows_of in zip(outs, groups):
            here = hidden[first : first + rows_of, :]
            out[...] = jnp.dot(here, down, preferred_element_type=jnp.float32).astype(out.dtype)
            first += rows_of


def experts(pieces, groups, scale, gate_weight, up_weight, down_weight):
    exp_local, width, ff = gate_weight.shape
    counts = [p.shape[0] for p in pieces]
    total = sum(counts)
    k_tile, d_tile = tile_of(width, 1024), tile_of(width, 1024)
    k_steps, d_steps = width // k_tile, width // d_tile
    at_k = lambda s: jnp.minimum(s, k_steps - 1)
    at_d = lambda s: jnp.maximum(s - k_steps, 0)
    in_specs = [pl.BlockSpec((c, k_tile), lambda s: (0, at_k(s))) for c in counts]
    in_specs += [
        pl.BlockSpec((total, exp_local), lambda s: (0, 0)),
        pl.BlockSpec((exp_local, k_tile, ff), lambda s: (0, at_k(s), 0)),
        pl.BlockSpec((exp_local, k_tile, ff), lambda s: (0, at_k(s), 0)),
        pl.BlockSpec((exp_local, ff, d_tile), lambda s: (0, 0, at_d(s))),
    ]
    weight_bytes = 2 * 3 * exp_local * width * ff
    return pl.pallas_call(
        functools.partial(expert_kernel, counts, groups, k_steps, d_steps),
        grid=(k_steps + d_steps,),
        in_specs=in_specs,
        out_specs=[pl.BlockSpec((g, d_tile), lambda s: (0, at_d(s))) for g in groups],
        out_shape=[jax.ShapeDtypeStruct((g, width), jnp.bfloat16) for g in groups],
        scratch_shapes=[
            pltpu.VMEM((exp_local, total, ff), jnp.float32),
            pltpu.VMEM((exp_local, total, ff), jnp.float32),
            pltpu.VMEM((total, exp_local * ff), jnp.bfloat16),
        ],
        compiler_params=pltpu.CompilerParams(
            dimension_semantics=("arbitrary",), vmem_limit_bytes=40 * 1024 * 1024
        ),
        cost_estimate=pl.CostEstimate(
            flops=6 * total * exp_local * width * ff,
            bytes_accessed=weight_bytes + 4 * total * width,
            transcendentals=total * exp_local * ff,
        ),
        name="experts",
    )(*pieces, scale, gate_weight, up_weight, down_weight)


def combine_table(gate_scores, expert_ids, experts_all):
    weights = 2.5 * gate_scores / jnp.sum(gate_scores, axis=1, keepdims=True)
    chosen = expert_ids[:, :, None] == jnp.arange(experts_all)[None, None, :]
    return jnp.sum(jnp.where(chosen, weights[:, :, None], 0.0), axis=1)


def add(a, b):
    return (a.astype(jnp.float32) + b.astype(jnp.float32)).astype(jnp.bfloat16)


def share_out(rows):
    n_tp = lax.axis_size("tp")
    me = lax.axis_index("tp")
    share = rows.shape[1] // n_tp
    take = lambda at: lax.dynamic_slice_in_dim(rows, at * share, share, axis=1)
    total = take(me).astype(jnp.float32)
    parts = []
    for k in reversed(range(1, n_tp)):
        perm = [(i, (i + k) % n_tp) for i in range(n_tp)]
        parts.append(lax.ppermute(take(lax.rem(me + k, n_tp)), "tp", perm))
    for part in parts:
        total = total + part.astype(jnp.float32)
    return total.astype(jnp.bfloat16)


def local_by_pairs(tokens, gate_scores, expert_ids, gate_weight, up_weight, down_weight):
    n_ep = lax.axis_size("ep")
    exp_local = gate_weight.shape[0]
    tok = tokens.shape[0]
    me = lax.axis_index("ep")
    pair = [(i, i ^ 1) for i in range(n_ep)]
    side = [(i, i ^ (4 if i % 2 else 2)) for i in range(n_ep)]
    cross = [(i, i ^ (2 if i % 2 else 4)) for i in range(n_ep)]
    send = lambda x, perm: lax.ppermute(x, "ep", perm)

    partner = send(tokens, pair)
    table = combine_table(gate_scores, expert_ids, exp_local * n_ep)
    table = lax.all_gather(table, "ep", axis=0)
    odd = lax.rem(me, 2)
    near, far = 2 + 2 * odd, 4 - 2 * odd
    sources = jnp.stack([far + 1, far, me * 0 + 7, near, near + 1, me * 0 + 6, me * 0, me * 0 + 1])
    table = lax.dynamic_slice_in_dim(table, me * exp_local, exp_local, axis=2)
    table = table[jnp.bitwise_xor(me, sources)]

    rows = tok // CHUNKS
    sent = []
    for j in range(CHUNKS):
        own, mate = (t[j * rows : (j + 1) * rows] for t in (tokens, partner))
        block = send(jnp.concatenate([own, mate], axis=0), side)
        sent.append((own, mate, block))
    results = []
    for j, (own, mate, block) in enumerate(sent):
        corner = send(block[:rows], cross)
        block_mate = send(block, pair)
        corner_mate = send(corner, pair)
        scale = table[:, j * rows : (j + 1) * rows].reshape(n_ep * rows, exp_local)
        away, kept_block, kept_corner, here, here_mate = experts(
            [block_mate, corner_mate, block, corner, own, mate],
            [3 * rows, 2 * rows, rows, rows, rows],
            scale, gate_weight, up_weight, down_weight,
        )
        away = send(away, pair)
        corner = send(add(kept_corner, away[2 * rows :]), cross)
        block_low = add(add(kept_block[:rows], away[:rows]), corner)
        block_high = add(kept_block[rows:], away[rows : 2 * rows])
        block = send(jnp.concatenate([block_low, block_high], axis=0), side)
        mate = send(add(here_mate, block[rows:]), pair)
        results.append(share_out(add(add(here, block[:rows]), mate)))
    return jnp.concatenate(results, axis=0)


def local(tokens, gate_scores, expert_ids, gate_weight, up_weight, down_weight):
    n_ep = lax.axis_size("ep")
    exp_local = gate_weight.shape[0]
    me = lax.axis_index("ep")
    table = combine_table(gate_scores, expert_ids, exp_local * n_ep)
    table = lax.all_gather(table, "ep", axis=0, tiled=True)
    table = lax.dynamic_slice_in_dim(table, me * exp_local, exp_local, axis=1)
    rows = lax.all_gather(tokens, "ep", axis=0, tiled=True)
    (partial,) = experts(
        [rows], [rows.shape[0]], table, gate_weight, up_weight, down_weight
    )
    summed = lax.psum_scatter(partial, "ep", scatter_dimension=0, tiled=True)
    return lax.psum_scatter(summed, "tp", scatter_dimension=1, tiled=True)


def solution(mesh):
    placed = (
        P("ep", None),
        P("ep", None),
        P("ep", None),
        P("ep", None, "tp"),
        P("ep", None, "tp"),
        P("ep", "tp", None),
    )
    body = local_by_pairs if mesh.shape["ep"] == 8 else local
    return jax.shard_map(
        body, mesh=mesh, in_specs=placed, out_specs=P("ep", "tp"), check_vma=False
    )
```

time: 419 us -> 178 us (0.42)
  waiting for transfers between devices: 215 us -> 62.8 us
  blocking collectives: 127 us -> 11.6 us
  Pallas kernels: 0 us -> 65.2 us
  matrix products: 34.7 us -> 0 us
  starting transfers between devices: 3.66 us -> 22.9 us
  local copies, waits for them, and re-layouts: 22.7 us -> 9.41 us
  between operations: 13.5 us -> 0.26 us
    reduce_scatter x1 -> x0, waiting for transfers between devices: 186 us -> none  [local(): lax.psum_scatter(rounded, 'tp', scatter_dimension=3, tiled=True)]
    all_to_all x1 -> x0, blocking collectives: 127 us -> none  [local(): lax.all_to_all(outgoing, 'ep', split_axis=0, concat_axis=0, tiled=True)]
    pallas_call x0 -> x2, Pallas kernels: none -> 65.2 us  [experts(): pl.pallas_call(functools.partial(expert_kernel, counts, groups, k_steps,...]
    ppermute x0 -> x23, waiting for transfers between devices: none -> 62.8 us  [the longest x17 47.2 us: local_by_pairs(): send = lambda x, perm: lax.ppermute(x, 'ep', perm)]
    dot_general x4 -> x0, matrix products: 34.7 us -> none  [the longest x1 13.9 us: local(): jnp.einsum('sjcf,jfd->sjcd', hidden, down_weight, preferred_element_type=...]
    all_to_all x1 -> x0, waiting for transfers between devices: 29.1 us -> none  [local(): lax.all_to_all(summed, 'ep', split_axis=0, concat_axis=0, tiled=True)]
    ppermute x0 -> x23, starting transfers between devices: none -> 22.9 us  [the longest x17 15.1 us: local_by_pairs(): send = lambda x, perm: lax.ppermute(x, 'ep', perm)]
    gather x7 -> x1, local copies, waits for them, and re-layouts: 16.7 us -> 0.58 us  [local_by_pairs(): table = table[jnp.bitwise_xor(me, sources)]]
  transfers between devices with their start and end apart: 2 -> 23, of which waited for: 2 -> 12; matrix products, arithmetic and copies ran while one was open for 1% -> 5% of each run, Pallas kernels for 0% -> 37%
where the time goes in v1:
time: 178 us
  Pallas kernels  65.2 us (37%)
  waiting for transfers between devices  62.8 us (35%)
  starting transfers between devices  22.9 us (13%)
  blocking collectives  11.6 us (7%)
  local copies, waits for them, and re-layouts  9.41 us (5%)
  other arithmetic  5.59 us (3%)
    pallas_call x2, Pallas kernels, experts(): pl.pallas_call(functools.partial(expert_kernel, counts, groups, k_steps,...  65.2 us
    ppermute x17, waiting for transfers between devices, local_by_pairs(): send = lambda x, perm: lax.ppermute(x, 'ep', perm)  47.2 us
    ppermute x6, waiting for transfers between devices, share_out(): parts.append(lax.ppermute(take(lax.rem(me + k, n_tp)), 'tp', perm))  15.7 us
    ppermute x17, starting transfers between devices, local_by_pairs(): send = lambda x, perm: lax.ppermute(x, 'ep', perm)  15.1 us
    all_gather x1, blocking collectives, local_by_pairs(): table = lax.all_gather(table, 'ep', axis=0)  11.6 us
    ppermute x6, starting transfers between devices, share_out(): parts.append(lax.ppermute(take(lax.rem(me + k, n_tp)), 'tp', perm))  7.77 us
    unnamed x24, local copies, waits for them, and re-layouts  5.4 us
  transfers between devices with their start and end apart: 23, of which 12 were waited for; matrix products, arithmetic and copies ran while one was open for 5% of the time, Pallas kernels for 37%

profile of v1, /device:TPU:0, one launch (start us, length us, event | category | flops | bytes accessed | tf_op | source)
XLA Modules:
  0.0 177.8 jit_solution(17207158872383035141)
XLA Ops:
  0.0 0.5 collective-permute-start
  0.5 1.2 fusion.1
  1.7 1.1 collective-permute-done
  2.9 2.9 %collective-permute-start.1 = (bf16[64,7168]{1,0:T(8,128)(2,1)S(1)}, bf16[64,7168]{1,0:T(8,128)(2,1)S(1)}, u32[]{:S(2)}, u32[]{:S(2)}) collective-permute-start(bf16[64,7168]{1,0:T(8,128)(2,1)S(1)} %pad_maximum_fusion), channel_id=1, source_target_pairs={{0,8},{4,20},{8,0},{12,28},{16,24},{20,4},{24,16},{28,12},{1,9},{5... | collective-permute-start | bytes 2752520 | tf_op jit(solution)/shard_map/ppermute | solution.py:131
  5.9 1.0 pad_maximum_fusion.2
  6.9 10.4 %collective-permute-done.1.refs_2_ = bf16[64,7168]{1,0:T(8,128)(2,1)S(1)} collective-permute-done((bf16[64,7168]{1,0:T(8,128)(2,1)S(1)}, bf16[64,7168]{1,0:T(8,128)(2,1)S(1)}, u32[]{:S(2)}, u32[]{:S(2)}) %collective-permute-start.1) | collective-permute-done | bytes 917536 | tf_op jit(solution)/shard_map/ppermute | solution.py:131
  17.2 0.9 copy-done
  18.2 0.8 slice.91
  19.0 2.0 %collective-permute-start.3 = (bf16[32,7168]{1,0:T(8,128)(2,1)}, bf16[32,7168]{1,0:T(8,128)(2,1)}, u32[]{:S(2)}, u32[]{:S(2)}) collective-permute-start(bf16[32,7168]{1,0:T(8,128)(2,1)} %slice.91), channel_id=1, source_target_pairs={{0,16},{4,12},{8,24},{12,4},{16,0},{20,28},{24,8},{28,20},{1,17},{... | collective-permute-start | bytes 1376264 | tf_op jit(solution)/shard_map/ppermute | solution.py:131
  21.2 10.8 %collective-permute-done.12.refs_2_ = bf16[64,7168]{1,0:T(8,128)(2,1)S(1)} collective-permute-done((bf16[64,7168]{1,0:T(8,128)(2,1)}, bf16[64,7168]{1,0:T(8,128)(2,1)S(1)}, u32[]{:S(2)}, u32[]{:S(2)}) %collective-permute-start.12) | collective-permute-done | bytes 917536 | tf_op jit(solution)/shard_map/ppermute | solution.py:131
  32.0 0.8 slice.99
  32.8 2.0 %collective-permute-start.14 = (bf16[32,7168]{1,0:T(8,128)(2,1)}, bf16[32,7168]{1,0:T(8,128)(2,1)S(1)}, u32[]{:S(2)}, u32[]{:S(2)}) collective-permute-start(bf16[32,7168]{1,0:T(8,128)(2,1)} %slice.99), channel_id=1, source_target_pairs={{0,16},{4,12},{8,24},{12,4},{16,0},{20,28},{24,8},{28,20},{1,17},{... | collective-permute-start | bytes 1376264 | tf_op jit(solution)/shard_map/ppermute | solution.py:131
  34.9 11.6 %all-gather.1 = f32[8,64,16]{1,2,0:T(8,128)S(1)} all-gather(f32[1,64,16]{1,2,0:T(8,128)S(1)} %bitcast.11), channel_id=2, replica_groups=mesh['ep'=8,'tp'=4] {'ep'}, dimensions={0}, use_global_device_ids=true | all-gather | bytes 36864 | tf_op jit(solution)/shard_map/all_gather | solution.py:135
  46.5 0.6 gather_fusion
  47.3 0.4 collective-permute-start.13
  47.7 0.1 collective-permute-start.15
  47.9 1.2 copy-done.1
  49.1 32.9 %experts.2 = (bf16[96,7168]{1,0:T(8,128)(2,1)}, bf16[64,7168]{1,0:T(8,128)(2,1)S(1)}, bf16[32,7168]{1,0:T(8,128)(2,1)S(1)}, bf16[32,7168]{1,0:T(8,128)(2,1)S(1)}, bf16[32,7168]{1,0:T(8,128)(2,1)S(1)}) custom-call(bf16[64,7168]{1,0:T(8,128)(2,1)} %collective-permute-done.2.refs_0_, bf16[32,7168]{1,0:T(8,128)(2,1)} %collective-permute-done.4.refs_1_, ...), custom_call_target="tpu_custom_call" | custom-call | flops 11274289152 | bytes 51380224 | tf_op jit(solution)/shard_map/experts/pallas_call | solution.py:75
  81.9 0.9 copy-done.2
  82.9 0.8 copy-done.4
  83.7 0.8 copy-done.6
  84.5 0.8 copy-done.8
  85.2 0.4 collective-permute-start.5
  85.7 32.4 %experts.3 = (bf16[96,7168]{1,0:T(8,128)(2,1)S(1)}, bf16[64,7168]{1,0:T(8,128)(2,1)S(1)}, bf16[32,7168]{1,0:T(8,128)(2,1)S(1)}, bf16[32,7168]{1,0:T(8,128)(2,1)S(1)}, bf16[32,7168]{1,0:T(8,128)(2,1)S(1)}) custom-call(bf16[64,7168]{1,0:T(8,128)(2,1)} %collective-permute-done.13.refs_0_, bf16[32,7168]{1,0:T(8,128)(2,1)} %collective-permute-done.15.refs_1_, ...), custom_call_target="tpu_custom_call" | custom-call | flops 11274289152 | bytes 51380224 | tf_op jit(solution)/shard_map/experts/pallas_call | solution.py:75
  118.1 0.2 collective-permute-start.16
  118.4 1.2 add_convert_fusion.12
  119.5 1.6 collective-permute-start.6
  121.1 0.2 collective-permute-done.16
  121.4 1.6 collective-permute-start.17
  123.0 5.1 %collective-permute-done.6 = bf16[32,7168]{1,0:T(8,128)(2,1)S(1)} collective-permute-done((bf16[32,7168]{1,0:T(8,128)(2,1)S(1)}, bf16[32,7168]{1,0:T(8,128)(2,1)S(1)}, u32[]{:S(2)}, u32[]{:S(2)}) %collective-permute-start.6) | collective-permute-done | bytes 458784 | tf_op jit(solution)/shard_map/ppermute | solution.py:131
  128.1 1.4 add_convert_fusion.11
  129.6 1.6 collective-permute-start.7
  131.1 3.1 %collective-permute-done.17 = bf16[32,7168]{1,0:T(8,128)(2,1)S(1)} collective-permute-done((bf16[32,7168]{1,0:T(8,128)(2,1)S(1)}, bf16[32,7168]{1,0:T(8,128)(2,1)S(1)}, u32[]{:S(2)}, u32[]{:S(2)}) %collective-permute-start.17) | collective-permute-done | bytes 458784 | tf_op jit(solution)/shard_map/ppermute | solution.py:131
  134.3 0.3 add_convert_fusion.4
  134.6 1.6 collective-permute-start.18
  136.2 6.8 %collective-permute-done.7 = bf16[64,7168]{1,0:T(8,128)(2,1)S(1)} collective-permute-done((bf16[64,7168]{1,0:T(8,128)(2,1)S(1)}, bf16[64,7168]{1,0:T(8,128)(2,1)S(1)}, u32[]{:S(2)}, u32[]{:S(2)}) %collective-permute-start.7) | collective-permute-done | bytes 917536 | tf_op jit(solution)/shard_map/ppermute | solution.py:131
  143.2 9.6 %collective-permute-done.18 = bf16[64,7168]{1,0:T(8,128)(2,1)S(1)} collective-permute-done((bf16[64,7168]{1,0:T(8,128)(2,1)S(1)}, bf16[64,7168]{1,0:T(8,128)(2,1)S(1)}, u32[]{:S(2)}, u32[]{:S(2)}) %collective-permute-start.18) | collective-permute-done | bytes 917536 | tf_op jit(solution)/shard_map/ppermute | solution.py:131
  153.1 0.2 add_convert_fusion.7
  153.3 2.7 %collective-permute-start.10 = (bf16[32,1792]{1,0:T(8,128)(2,1)S(1)}, bf16[32,1792]{1,0:T(8,128)(2,1)S(1)}, u32[]{:S(2)}, u32[]{:S(2)}) collective-permute-start(bf16[32,1792]{1,0:T(8,128)(2,1)S(1)} %get-tuple-element.35), channel_id=1, source_target_pairs={{0,2},{1,3},{2,0},{3,1},{4,6},{5,7},{6,4},{7,5},{8,10},{9,11},{10,... | collective-permute-start | bytes 344072 | tf_op jit(solution)/shard_map/ppermute | solution.py:117
  156.0 1.6 collective-permute-start.11
  157.5 2.2 %collective-permute-start.9 = (bf16[32,1792]{1,0:T(8,128)(2,1)S(1)}, bf16[32,1792]{1,0:T(8,128)(2,1)S(1)}, u32[]{:S(2)}, u32[]{:S(2)}) collective-permute-start(bf16[32,1792]{1,0:T(8,128)(2,1)S(1)} %get-tuple-element.33), channel_id=1, source_target_pairs={{0,3},{1,0},{2,1},{3,2},{4,7},{5,4},{6,5},{7,6},{8,11},{9,8},{10,9... | collective-permute-start | bytes 344072 | tf_op jit(solution)/shard_map/ppermute | solution.py:117
  159.8 0.2 add_convert_fusion
  160.1 1.2 collective-permute-start.21
  161.3 3.9 %collective-permute-done.10 = bf16[32,1792]{1,0:T(8,128)(2,1)S(1)} collective-permute-done((bf16[32,1792]{1,0:T(8,128)(2,1)S(1)}, bf16[32,1792]{1,0:T(8,128)(2,1)S(1)}, u32[]{:S(2)}, u32[]{:S(2)}) %collective-permute-start.10) | collective-permute-done | bytes 114720 | tf_op jit(solution)/shard_map/ppermute | solution.py:117
  165.2 1.9 %collective-permute-done.9 = bf16[32,1792]{1,0:T(8,128)(2,1)S(1)} collective-permute-done((bf16[32,1792]{1,0:T(8,128)(2,1)S(1)}, bf16[32,1792]{1,0:T(8,128)(2,1)S(1)}, u32[]{:S(2)}, u32[]{:S(2)}) %collective-permute-start.9) | collective-permute-done | bytes 114720 | tf_op jit(solution)/shard_map/ppermute | solution.py:117
  167.2 1.6 collective-permute-done.20
  168.8 8.3 %collective-permute-done.21 = bf16[32,1792]{1,0:T(8,128)(2,1)S(1)} collective-permute-done((bf16[32,1792]{1,0:T(8,128)(2,1)S(1)}, bf16[32,1792]{1,0:T(8,128)(2,1)S(1)}, u32[]{:S(2)}, u32[]{:S(2)}) %collective-permute-start.21) | collective-permute-done | bytes 114720 | tf_op jit(solution)/shard_map/ppermute | solution.py:117
  177.1 0.7 pad_maximum_fusion.4
  (57 shorter events, 1.6 us)
Async XLA Ops:
  0.0 2.8 %collective-permute-start = (bf16[64,7168]{1,0:T(8,128)(2,1)}, bf16[64,7168]{1,0:T(8,128)(2,1)S(1)}, u32[]{:S(2)}, u32[]{:S(2)}) collective-permute-start(bf16[64,7168]{1,0:T(8,128)(2,1)} %param.6), channel_id=1, source_target_pairs={{0,4},{4,0},{8,12},{12,8},{16,20},{20,16},{24,28},{28,24},{1,5},{5... | collective-permute-start | bytes 2752520 | tf_op jit(solution)/shard_map/ppermute | solution.py:131
  2.9 18.1 %copy-start.10 = (f32[64,8]{0,1:T(8,128)S(1)}, f32[64,8]{0,1:T(8,128)}, u32[]{:S(2)}) copy-start(f32[64,8]{0,1:T(8,128)} %param.7) | copy-start | bytes 6148
  2.9 14.3 %collective-permute-start.1 = (bf16[64,7168]{1,0:T(8,128)(2,1)S(1)}, bf16[64,7168]{1,0:T(8,128)(2,1)S(1)}, u32[]{:S(2)}, u32[]{:S(2)}) collective-permute-start(bf16[64,7168]{1,0:T(8,128)(2,1)S(1)} %pad_maximum_fusion), channel_id=1, source_target_pairs={{0,8},{4,20},{8,0},{12,28},{16,24},{20,4},{24,16},{28,12},{1,9},{5... | collective-permute-start | bytes 2752520 | tf_op jit(solution)/shard_map/ppermute | solution.py:131
  5.9 29.0 %copy-start.11 = (s32[64,8]{0,1:T(8,128)S(1)}, s32[64,8]{0,1:T(8,128)}, u32[]{:S(2)}) copy-start(s32[64,8]{0,1:T(8,128)} %param.8) | copy-start | bytes 6148
  6.9 25.1 %collective-permute-start.12 = (bf16[64,7168]{1,0:T(8,128)(2,1)}, bf16[64,7168]{1,0:T(8,128)(2,1)S(1)}, u32[]{:S(2)}, u32[]{:S(2)}) collective-permute-start(bf16[64,7168]{1,0:T(8,128)(2,1)} %pad_maximum_fusion.2), channel_id=1, source_target_pairs={{0,8},{4,20},{8,0},{12,28},{16,24},{20,4},{24,16},{28,12},{1,9},{5... | collective-permute-start | bytes 2752520 | tf_op jit(solution)/shard_map/ppermute | solution.py:131
  17.2 0.9 copy-start
  19.0 15.9 %collective-permute-start.3 = (bf16[32,7168]{1,0:T(8,128)(2,1)}, bf16[32,7168]{1,0:T(8,128)(2,1)}, u32[]{:S(2)}, u32[]{:S(2)}) collective-permute-start(bf16[32,7168]{1,0:T(8,128)(2,1)} %slice.91), channel_id=1, source_target_pairs={{0,16},{4,12},{8,24},{12,4},{16,0},{20,28},{24,8},{28,20},{1,17},{... | collective-permute-start | bytes 1376264 | tf_op jit(solution)/shard_map/ppermute | solution.py:131
  21.2 26.7 %collective-permute-start.2 = (bf16[64,7168]{1,0:T(8,128)(2,1)}, bf16[64,7168]{1,0:T(8,128)(2,1)}, u32[]{:S(2)}, u32[]{:S(2)}) collective-permute-start(bf16[64,7168]{1,0:T(8,128)(2,1)} %copy-done), channel_id=1, source_target_pairs={{0,4},{4,0},{8,12},{12,8},{16,20},{20,16},{24,28},{28,24},{1,5},{5... | collective-permute-start | bytes 2752520 | tf_op jit(solution)/shard_map/ppermute | solution.py:131
  32.8 14.9 %collective-permute-start.14 = (bf16[32,7168]{1,0:T(8,128)(2,1)}, bf16[32,7168]{1,0:T(8,128)(2,1)S(1)}, u32[]{:S(2)}, u32[]{:S(2)}) collective-permute-start(bf16[32,7168]{1,0:T(8,128)(2,1)} %slice.99), channel_id=1, source_target_pairs={{0,16},{4,12},{8,24},{12,4},{16,0},{20,28},{24,8},{28,20},{1,17},{... | collective-permute-start | bytes 1376264 | tf_op jit(solution)/shard_map/ppermute | solution.py:131
  34.9 13.0 %collective-permute-start.4 = (bf16[32,7168]{1,0:T(8,128)(2,1)}, bf16[32,7168]{1,0:T(8,128)(2,1)}, u32[]{:S(2)}, u32[]{:S(2)}) collective-permute-start(bf16[32,7168]{1,0:T(8,128)(2,1)} %collective-permute-done.3.refs_3_), channel_id=1, source_target_pairs={{0,4},{4,0},{8,12},{12,8},{16,20},{20,16},{24,28},{28,24},{1,5},{5... | collective-permute-start | bytes 1376264 | tf_op jit(solution)/shard_map/ppermute | solution.py:131
  47.3 38.4 %collective-permute-start.13 = (bf16[64,7168]{1,0:T(8,128)(2,1)S(1)}, bf16[64,7168]{1,0:T(8,128)(2,1)}, u32[]{:S(2)}, u32[]{:S(2)}) collective-permute-start(bf16[64,7168]{1,0:T(8,128)(2,1)S(1)} %collective-permute-done.12.refs_2_), channel_id=1, source_target_pairs={{0,4},{4,0},{8,12},{12,8},{16,20},{20,16},{24,28},{28,24},{1,5},{5... | collective-permute-start | bytes 2752520 | tf_op jit(solution)/shard_map/ppermute | solution.py:131
  47.7 38.0 %collective-permute-start.15 = (bf16[32,7168]{1,0:T(8,128)(2,1)S(1)}, bf16[32,7168]{1,0:T(8,128)(2,1)}, u32[]{:S(2)}, u32[]{:S(2)}) collective-permute-start(bf16[32,7168]{1,0:T(8,128)(2,1)S(1)} %collective-permute-done.14.refs_3_), channel_id=1, source_target_pairs={{0,4},{4,0},{8,12},{12,8},{16,20},{20,16},{24,28},{28,24},{1,5},{5... | collective-permute-start | bytes 1376264 | tf_op jit(solution)/shard_map/ppermute | solution.py:131
  47.9 1.2 copy-start.1
  81.9 0.9 copy-start.2
  82.9 0.8 copy-start.4
  83.7 0.8 copy-start.6
  84.5 0.8 copy-start.8
  85.2 33.1 %collective-permute-start.5 = (bf16[96,7168]{1,0:T(8,128)(2,1)}, bf16[96,7168]{1,0:T(8,128)(2,1)}, u32[]{:S(2)}, u32[]{:S(2)}) collective-permute-start(bf16[96,7168]{1,0:T(8,128)(2,1)} %get-tuple-element.17), channel_id=1, source_target_pairs={{0,4},{4,0},{8,12},{12,8},{16,20},{20,16},{24,28},{28,24},{1,5},{5... | collective-permute-start | bytes 4128776 | tf_op jit(solution)/shard_map/ppermute | solution.py:131
  85.7 32.6 %copy-start.9 = (bf16[32,7168]{1,0:T(8,128)(2,1)S(1)}, bf16[32,7168]{1,0:T(8,128)(2,1)}, u32[]{:S(2)}) copy-start(bf16[32,7168]{1,0:T(8,128)(2,1)} %copy-done.8) | copy-start | bytes 1376260
  118.1 10.0 %copy-start.3 = (bf16[64,7168]{1,0:T(8,128)(2,1)S(1)}, bf16[64,7168]{1,0:T(8,128)(2,1)}, u32[]{:S(2)}) copy-start(bf16[64,7168]{1,0:T(8,128)(2,1)} %copy-done.2) | copy-start | bytes 2752516
  118.1 3.2 %collective-permute-start.16 = (bf16[96,7168]{1,0:T(8,128)(2,1)S(1)}, bf16[96,7168]{1,0:T(8,128)(2,1)S(1)}, u32[]{:S(2)}, u32[]{:S(2)}) collective-permute-start(bf16[96,7168]{1,0:T(8,128)(2,1)S(1)} %get-tuple-element.22), channel_id=1, source_target_pairs={{0,4},{4,0},{8,12},{12,8},{16,20},{20,16},{24,28},{28,24},{1,5},{5... | collective-permute-start | bytes 4128776 | tf_op jit(solution)/shard_map/ppermute | solution.py:131
  119.5 8.5 %collective-permute-start.6 = (bf16[32,7168]{1,0:T(8,128)(2,1)S(1)}, bf16[32,7168]{1,0:T(8,128)(2,1)S(1)}, u32[]{:S(2)}, u32[]{:S(2)}) collective-permute-start(bf16[32,7168]{1,0:T(8,128)(2,1)S(1)} %add_convert_fusion.12), channel_id=1, source_target_pairs={{0,16},{4,12},{8,24},{12,4},{16,0},{20,28},{24,8},{28,20},{1,17},{... | collective-permute-start | bytes 1376264 | tf_op jit(solution)/shard_map/ppermute | solution.py:131
  121.4 12.8 %collective-permute-start.17 = (bf16[32,7168]{1,0:T(8,128)(2,1)S(1)}, bf16[32,7168]{1,0:T(8,128)(2,1)S(1)}, u32[]{:S(2)}, u32[]{:S(2)}) collective-permute-start(bf16[32,7168]{1,0:T(8,128)(2,1)S(1)} %add_convert_fusion.5), channel_id=1, source_target_pairs={{0,16},{4,12},{8,24},{12,4},{16,0},{20,28},{24,8},{28,20},{1,17},{... | collective-permute-start | bytes 1376264 | tf_op jit(solution)/shard_map/ppermute | solution.py:131
  129.6 13.5 %collective-permute-start.7 = (bf16[64,7168]{1,0:T(8,128)(2,1)S(1)}, bf16[64,7168]{1,0:T(8,128)(2,1)S(1)}, u32[]{:S(2)}, u32[]{:S(2)}) collective-permute-start(bf16[64,7168]{1,0:T(8,128)(2,1)S(1)} %pad_maximum_fusion.1), channel_id=1, source_target_pairs={{0,8},{4,20},{8,0},{12,28},{16,24},{20,4},{24,16},{28,12},{1,9},{5... | collective-permute-start | bytes 2752520 | tf_op jit(solution)/shard_map/ppermute | solution.py:131
  134.3 8.8 %copy-start.7 = (bf16[32,7168]{1,0:T(8,128)(2,1)S(1)}, bf16[32,7168]{1,0:T(8,128)(2,1)}, u32[]{:S(2)}) copy-start(bf16[32,7168]{1,0:T(8,128)(2,1)} %copy-done.6) | copy-start | bytes 1376260
  134.6 18.4 %copy-start.5 = (bf16[32,7168]{1,0:T(8,128)(2,1)S(1)}, bf16[32,7168]{1,0:T(8,128)(2,1)}, u32[]{:S(2)}) copy-start(bf16[32,7168]{1,0:T(8,128)(2,1)} %copy-done.4) | copy-start | bytes 1376260
  134.6 18.2 %collective-permute-start.18 = (bf16[64,7168]{1,0:T(8,128)(2,1)S(1)}, bf16[64,7168]{1,0:T(8,128)(2,1)S(1)}, u32[]{:S(2)}, u32[]{:S(2)}) collective-permute-start(bf16[64,7168]{1,0:T(8,128)(2,1)S(1)} %pad_maximum_fusion.3), channel_id=1, source_target_pairs={{0,8},{4,20},{8,0},{12,28},{16,24},{20,4},{24,16},{28,12},{1,9},{5... | collective-permute-start | bytes 2752520 | tf_op jit(solution)/shard_map/ppermute | solution.py:131
  143.2 9.9 %collective-permute-start.8 = (bf16[32,7168]{1,0:T(8,128)(2,1)S(1)}, bf16[32,7168]{1,0:T(8,128)(2,1)S(1)}, u32[]{:S(2)}, u32[]{:S(2)}) collective-permute-start(bf16[32,7168]{1,0:T(8,128)(2,1)S(1)} %add_convert_fusion.8), channel_id=1, source_target_pairs={{0,4},{4,0},{8,12},{12,8},{16,20},{20,16},{24,28},{28,24},{1,5},{5... | collective-permute-start | bytes 1376264 | tf_op jit(solution)/shard_map/ppermute | solution.py:131
  153.0 6.8 %collective-permute-start.19 = (bf16[32,7168]{1,0:T(8,128)(2,1)S(1)}, bf16[32,7168]{1,0:T(8,128)(2,1)S(1)}, u32[]{:S(2)}, u32[]{:S(2)}) collective-permute-start(bf16[32,7168]{1,0:T(8,128)(2,1)S(1)} %add_convert_fusion.1), channel_id=1, source_target_pairs={{0,4},{4,0},{8,12},{12,8},{16,20},{20,16},{24,28},{28,24},{1,5},{5... | collective-permute-start | bytes 1376264 | tf_op jit(solution)/shard_map/ppermute | solution.py:131
  153.3 11.9 %collective-permute-start.10 = (bf16[32,1792]{1,0:T(8,128)(2,1)S(1)}, bf16[32,1792]{1,0:T(8,128)(2,1)S(1)}, u32[]{:S(2)}, u32[]{:S(2)}) collective-permute-start(bf16[32,1792]{1,0:T(8,128)(2,1)S(1)} %get-tuple-element.35), channel_id=1, source_target_pairs={{0,2},{1,3},{2,0},{3,1},{4,6},{5,7},{6,4},{7,5},{8,10},{9,11},{10,... | collective-permute-start | bytes 344072 | tf_op jit(solution)/shard_map/ppermute | solution.py:117
  156.0 9.3 %collective-permute-start.11 = (bf16[32,1792]{1,0:T(8,128)(2,1)S(1)}, bf16[32,1792]{1,0:T(8,128)(2,1)S(1)}, u32[]{:S(2)}, u32[]{:S(2)}) collective-permute-start(bf16[32,1792]{1,0:T(8,128)(2,1)S(1)} %get-tuple-element.34), channel_id=1, source_target_pairs={{0,1},{1,2},{2,3},{3,0},{4,5},{5,6},{6,7},{7,4},{8,9},{9,10},{10,1... | collective-permute-start | bytes 344072 | tf_op jit(solution)/shard_map/ppermute | solution.py:117
  157.5 9.6 %collective-permute-start.9 = (bf16[32,1792]{1,0:T(8,128)(2,1)S(1)}, bf16[32,1792]{1,0:T(8,128)(2,1)S(1)}, u32[]{:S(2)}, u32[]{:S(2)}) collective-permute-start(bf16[32,1792]{1,0:T(8,128)(2,1)S(1)} %get-tuple-element.33), channel_id=1, source_target_pairs={{0,3},{1,0},{2,1},{3,2},{4,7},{5,4},{6,5},{7,6},{8,11},{9,8},{10,9... | collective-permute-start | bytes 344072 | tf_op jit(solution)/shard_map/ppermute | solution.py:117
  160.0 8.8 %collective-permute-start.20 = (bf16[32,1792]{1,0:T(8,128)(2,1)S(1)}, bf16[32,1792]{1,0:T(8,128)(2,1)S(1)}, u32[]{:S(2)}, u32[]{:S(2)}) collective-permute-start(bf16[32,1792]{1,0:T(8,128)(2,1)S(1)} %get-tuple-element.36), channel_id=1, source_target_pairs={{0,3},{1,0},{2,1},{3,2},{4,7},{5,4},{6,5},{7,6},{8,11},{9,8},{10,9... | collective-permute-start | bytes 344072 | tf_op jit(solution)/shard_map/ppermute | solution.py:117
  160.1 17.0 %collective-permute-start.21 = (bf16[32,1792]{1,0:T(8,128)(2,1)S(1)}, bf16[32,1792]{1,0:T(8,128)(2,1)S(1)}, u32[]{:S(2)}, u32[]{:S(2)}) collective-permute-start(bf16[32,1792]{1,0:T(8,128)(2,1)S(1)} %get-tuple-element.38), channel_id=1, source_target_pairs={{0,2},{1,3},{2,0},{3,1},{4,6},{5,7},{6,4},{7,5},{8,10},{9,11},{10,... | collective-permute-start | bytes 344072 | tf_op jit(solution)/shard_map/ppermute | solution.py:117
  165.2 11.8 %collective-permute-start.22 = (bf16[32,1792]{1,0:T(8,128)(2,1)S(1)}, bf16[32,1792]{1,0:T(8,128)(2,1)S(1)}, u32[]{:S(2)}, u32[]{:S(2)}) collective-permute-start(bf16[32,1792]{1,0:T(8,128)(2,1)S(1)} %get-tuple-element.37), channel_id=1, source_target_pairs={{0,1},{1,2},{2,3},{3,0},{4,5},{5,6},{6,7},{7,4},{8,9},{9,10},{10,1... | collective-permute-start | bytes 344072 | tf_op jit(solution)/shard_map/ppermute | solution.py:117
